TPU v7x, 32 devices: a whole 2x2x4 slice. The times are simulated.
32 devices in a mesh: rows: 8 (over z, x), grp: 4 (over y, core).
Axes of the slice: x: 2, y: 2, z: 4, core: 2. Of those that a mesh axis runs over, the one named last changes fastest.
Arguments:
- tile_values: bfloat16 [1024, 16, 128], P('rows'), may hold values from 0.049804688 to 1
- tile_ids: int32 [1024, 16], P('rows'), may hold values from 0 to 255, as said below
- doc_tiles: int32 [1024], P('rows'), may hold values from 1 to 16
- row_counts: int32 [8], replicated, may hold values from 1 to 128, 512 in all
Outputs:
- similarity: float32 [512, 512], P('rows', 'grp')
Inputs may be any that keep to these rules, and one draw needn't show every extreme that they name: `row_counts`: the entries sum to 512. `tile_ids`: the 16 entries of a row are distinct.
All inputs are finite; a program needn't handle non-finite values.
Results may differ from a plain program's by a relative error of at most 0.0003.
Values may be sent and summed in bfloat16 or wider, within the bound.
A program may use at most 64 MiB of HBM per device.

v0:
```python
import jax
import jax.numpy as jnp
from jax import lax
from jax.sharding import PartitionSpec as P

VOCAB = 32768
TILE = 128
LTILES = 16
DOC_DEV = 64


def from_behind(block, axis, distance):
    devices = range(lax.axis_size(axis))
    route = [((i - distance) % len(devices), i) for i in devices]
    return lax.ppermute(block, axis, route)


def densify(values, tile_codes):
    doc_count = values.shape[0]
    tile_count = VOCAB // TILE
    tile_line = jnp.arange(tile_count, dtype=jnp.int32)[None, None, :]
    selector = (tile_codes.astype(jnp.int32)[:, :, None] == tile_line).astype(jnp.bfloat16)
    placed = jnp.einsum("dkt,dki->dti", selector, values, preferred_element_type=jnp.float32)
    return placed.astype(jnp.bfloat16).reshape(doc_count, VOCAB)


def squares(values):
    widened = values.astype(jnp.float32)
    return jnp.sum(widened * widened, axis=(1, 2))


def similar(own_dense, own_norms, values, tile_codes):
    other_dense = densify(values, tile_codes)
    product = lax.dot_general(
        own_dense, other_dense, (((1,), (1,)), ((), ())), preferred_element_type=jnp.float32
    )
    return product / (own_norms[:, None] + squares(values)[None, :] - product)


def forward(values, tile_codes):
    return from_behind((values, tile_codes), "rows", 1)


def deal(tile_values, tile_ids, doc_tiles, row_counts, offsets):
    capacity = tile_values.shape[0]
    rank_count = lax.axis_size("rows")
    here_rank = lax.axis_index("rows")
    slot_count = (capacity + rank_count - 1) // rank_count
    run_ends = jnp.cumsum(row_counts)
    run_starts = run_ends - row_counts
    own_start = run_starts[here_rank]
    own_count = row_counts[here_rank]
    live_mask = jnp.arange(LTILES, dtype=jnp.int32)[None, :] < doc_tiles[:, None]
    masked = jnp.where(live_mask[:, :, None], tile_values, jnp.zeros_like(tile_values))
    target_ids = jnp.arange(rank_count, dtype=jnp.int32)[:, None]
    slot_ids = jnp.arange(slot_count, dtype=jnp.int32)[None, :]
    chosen = (target_ids - own_start) % rank_count + slot_ids * rank_count
    usable = chosen < own_count
    chosen = jnp.where(usable, chosen, 0)
    outgoing = jnp.where(usable[:, :, None, None], masked[chosen], jnp.zeros((), jnp.bfloat16))
    out_codes = tile_ids[chosen].astype(jnp.bfloat16)
    outgoing = jnp.concatenate([jnp.roll(outgoing, offset, axis=0) for offset in offsets], axis=1)
    out_codes = jnp.concatenate([jnp.roll(out_codes, offset, axis=0) for offset in offsets], axis=1)
    incoming, in_codes = (
        lax.all_to_all(outgoing, "rows", split_axis=0, concat_axis=0, tiled=True),
        lax.all_to_all(out_codes, "rows", split_axis=0, concat_axis=0, tiled=True),
    )
    panel_line = jnp.arange(DOC_DEV, dtype=jnp.int32)[:, None]
    panels = []
    for number, offset in enumerate(offsets):
        anchor = (here_rank - offset) % rank_count
        first_row = (anchor - run_starts[:, None]) % rank_count + slot_ids * rank_count
        landed = first_row < row_counts[:, None]
        places = jnp.where(
            landed, (run_starts[:, None] + first_row) // rank_count, DOC_DEV
        ).reshape(-1)
        block_values = incoming[:, number * slot_count : (number + 1) * slot_count].reshape(
            -1, LTILES, TILE
        )
        block_codes = in_codes[:, number * slot_count : (number + 1) * slot_count].reshape(
            -1, LTILES
        )
        placing = (places[None, :] == panel_line).astype(jnp.bfloat16)
        values = jnp.einsum(
            "pn,nki->pki", placing, block_values, preferred_element_type=jnp.float32
        ).astype(jnp.bfloat16)
        codes = jnp.einsum(
            "pn,nk->pk", placing, block_codes, preferred_element_type=jnp.float32
        ).astype(jnp.bfloat16)
        panels.append((values, codes))
    return panels


def on_device(tile_values, tile_ids, doc_tiles, row_counts):
    panel_span = lax.axis_size("rows") // lax.axis_size("grp")
    group_index = lax.axis_index("grp")
    lead_offset = group_index * panel_span
    zero_offset = jnp.zeros((), jnp.int32)
    offsets = [zero_offset, lead_offset]
    panels = deal(tile_values, tile_ids, doc_tiles, row_counts, offsets)
    own_values, own_codes = panels[0]
    own_dense = densify(own_values, own_codes)
    own_norms = squares(own_values)
    output = jnp.zeros((DOC_DEV, panel_span * DOC_DEV), jnp.float32)

    def record(output, column_block, values, codes):
        block = similar(own_dense, own_norms, values, codes)
        return lax.dynamic_update_slice_in_dim(output, block, column_block * DOC_DEV, 1)

    def turn_one(counter, carry):
        output, ahead_values, ahead_codes = carry
        output = record(output, counter, ahead_values, ahead_codes)
        ahead_values, ahead_codes = forward(ahead_values, ahead_codes)
        return (output, ahead_values, ahead_codes)

    start_carry = (output, panels[1][0], panels[1][1])
    output, ahead_values, ahead_codes = lax.fori_loop(0, panel_span - 1, turn_one, start_carry)
    output = record(output, panel_span - 1, ahead_values, ahead_codes)
    return output


def solution(mesh):
    placed = (P("rows", None, None), P("rows", None), P("rows"), P())
    return jax.shard_map(
        on_device, mesh=mesh, in_specs=placed, out_specs=P("rows", "grp"), check_vma=False
    )
```

profile of v0, /device:TPU:0, one launch (start us, length us, event | category | flops | bytes accessed | tf_op | source)
XLA Modules:
  0.0 73.1 jit_solution(9646442547085822986)
XLA Ops:
  0.0 0.8 %reduce-window.9 = s32[8,1]{0,1:T(1,128)S(1)} reduce-window(s32[8,1]{0,1:T(1,128)} %bitcast.44, s32[]{:T(128)} %constant.148.clone.1), window={size=8x1 pad=7_0x0_0}, to_apply=%region_0.0 | reduce-window | flops 56 | bytes 68 | tf_op jit(solution)/shard_map/reduce-window.4
  0.8 1.3 %dynamic_slice.17 = s32[1]{0:T(128)} dynamic-slice(s32[8]{0:T(128)} %param.15, s32[]{:T(128)S(6)} %select_n.124), dynamic_slice_sizes={1} | dynamic-slice | bytes 12 | tf_op jit(solution)/shard_map/dynamic_slice | solution.py:52
  2.1 0.7 and_select_fusion.4
  2.8 0.6 dynamic_slice.16
  3.4 0.7 and_select_fusion.1
  4.0 0.7 compare_select_fusion
  4.7 0.1 reshape.300
  4.8 0.8 %copy.23 = s32[128,16]{1,0:T(8,128)S(1)} copy(s32[128,16]{0,1:T(8,128)} %param.13) | data formatting | bytes 16384 | tf_op args[1]
  5.6 0.6 gather_fusion
  6.2 0.1 copy.26
  6.4 0.1 fusion.45
  6.5 0.7 reshape.321
  7.2 7.3 %all-to-all-start = ((bf16[8,2,256]{2,1,0:T(2,128)(2,1)}), bf16[8,2,256]{2,1,0:T(2,128)(2,1)S(1)}, u32[]{:S(2)}, u32[]{:S(2)}) async-start(bf16[8,2,256]{2,1,0:T(2,128)(2,1)} %reshape.321), calls=%async_computation | async-start | bytes 16384 | tf_op jit(solution)/shard_map/all_to_all | solution.py:66
  14.5 0.7 %iota_compare_fusion.6 = pred[128,16]{1,0:T(8,128)(4,1)S(1)} fusion(s32[128]{0:T(128)} %param.14), kind=kLoop, calls=%fused_computation.38 | loop fusion | flops 2048 | bytes 2560 | tf_op jit(solution)/shard_map/lt | solution.py:53
  15.2 1.4 %broadcast_select_fusion = bf16[128,16,128]{2,1,0:T(8,128)(2,1)S(1)} fusion(bf16[128,16,128]{2,1,0:T(8,128)(2,1)} %param.12, pred[128,16]{1,0:T(8,128)(4,1)S(1)} %iota_compare_fusion.6), kind=kLoop, calls=%fused_computation.31 | loop fusion | flops 262144 | bytes 1050624 | tf_op jit(solution)/shard_map/jit(_where)/select_n | solution.py:54
  16.6 0.7 gather_fusion.1
  17.3 1.3 %add_compare_fusion.1 = (pred[8,16]{1,0:T(8,128)(4,1)S(1)}, pred[8,16]{1,0:T(8,128)(4,1)S(1)}, pred[8,16]{1,0:T(8,128)(4,1)S(1)}) fusion(s32[8]{0:T(128)} %param.15, s32[16]{0:T(128)S(1)} %iota_multiply_fusion, s32[8]{0:T(128)S(1)} %get-tuple-element.28, s32[8]{0:T(128)S(1)} %get-tuple-element.47, s32[]{:T(128)} %bitcast.3, s32[8]{0:T(128)S(1)} %get-tuple-element.48), kind=kLoop, calls=%fused_computation.57 | loop fusion | flops 768 | bytes 580 | tf_op jit(solution)/shard_map/lt | solution.py:73
  18.7 0.2 broadcast_select_fusion.1
  18.9 0.2 fusion.17
  19.1 0.1 pad_maximum_fusion
  19.2 1.2 %copy.29 = bf16[8,32,16,128]{3,1,2,0:T(8,128)(2,1)} copy(bf16[8,32,16,128]{3,2,1,0:T(8,128)(2,1)S(1)} %pad_maximum_fusion) | data formatting | bytes 2097152 | tf_op jit(solution)/shard_map/concatenate | solution.py:62
  20.4 0.6 all-to-all-done
  21.0 5.4 %all-to-all-start.1 = ((bf16[8,32,16,128]{3,1,2,0:T(8,128)(2,1)}), bf16[8,32,16,128]{3,1,2,0:T(8,128)(2,1)S(1)}, u32[]{:S(2)}, u32[]{:S(2)}) async-start(bf16[8,32,16,128]{3,1,2,0:T(8,128)(2,1)} %copy.29), calls=%async_computation.1 | async-start | bytes 2097152 | tf_op jit(solution)/shard_map/all_to_all | solution.py:65
  26.4 0.1 lt.128
  26.7 0.1 lt.141
  26.9 0.1 reshape.322
  27.0 0.1 fusion.43
  27.1 0.1 reshape.294
  27.2 0.1 reshape.296
  27.3 0.1 fusion.44
  27.4 2.0 %collective-permute-start = (bf16[64,16]{0,1:T(8,128)(2,1)S(1)}, bf16[64,16]{0,1:T(8,128)(2,1)S(1)}, u32[]{:S(2)}, u32[]{:S(2)}) collective-permute-start(bf16[64,16]{0,1:T(8,128)(2,1)S(1)} %get-tuple-element.44), channel_id=1, source_target_pairs={{28,0},{0,4},{4,8},{8,12},{12,16},{16,20},{20,24},{24,28},{29,1},{... | collective-permute-start | bytes 6152 | tf_op jit(solution)/shard_map/while/body/eval_jaxpr/ppermute | solution.py:15
  29.4 0.1 fusion.16
  29.6 0.1 copy.28
  29.7 0.1 copy.33
  29.7 18.2 %collective-permute-done = bf16[64,16]{0,1:T(8,128)(2,1)S(1)} collective-permute-done((bf16[64,16]{0,1:T(8,128)(2,1)S(1)}, bf16[64,16]{0,1:T(8,128)(2,1)S(1)}, u32[]{:S(2)}, u32[]{:S(2)}) %collective-permute-start) | collective-permute-done | bytes 2080 | tf_op jit(solution)/shard_map/while/body/eval_jaxpr/ppermute | solution.py:15
  48.0 0.1 copy.38
  48.1 3.8 %all-to-all-done.1 = bf16[8,32,16,128]{3,1,2,0:T(8,128)(2,1)S(1)} async-done(((bf16[8,32,16,128]{3,1,2,0:T(8,128)(2,1)}), bf16[8,32,16,128]{3,1,2,0:T(8,128)(2,1)S(1)}, u32[]{:S(2)}, u32[]{:S(2)}) %all-to-all-start.1) | async-done | bytes 1048608 | tf_op jit(solution)/shard_map/all_to_all | solution.py:65
  51.9 0.3 fusion.42
  52.2 0.3 multiply_reduce_fusion.2
  52.6 0.3 multiply_reduce_fusion.1
  52.9 1.5 %collective-permute-start.1 = (bf16[64,16,128]{2,0,1:T(8,128)(2,1)S(1)}, bf16[64,16,128]{2,0,1:T(8,128)(2,1)S(1)}, u32[]{:S(2)}, u32[]{:S(2)}) collective-permute-start(bf16[64,16,128]{2,0,1:T(8,128)(2,1)S(1)} %get-tuple-element.46), channel_id=1, source_target_pairs={{28,0},{0,4},{4,8},{8,12},{12,16},{16,20},{20,24},{24,28},{29,1},{... | collective-permute-start | bytes 786440 | tf_op jit(solution)/shard_map/while/body/eval_jaxpr/ppermute | solution.py:15
  54.4 2.7 %convolution_convert_fusion.1 = bf16[64,256,128]{2,1,0:T(8,128)(2,1)S(1)} fusion(s32[64,16]{1,0:T(8,128)S(1)} %copy.33, bf16[64,16,128]{2,0,1:T(8,128)(2,1)S(1)} %get-tuple-element.46), kind=kOutput, calls=%fused_computation.9 | convolution fusion | flops 69468160 | bytes 4460544 | tf_op jit(solution)/shard_map/while/body/eval_jaxpr/dkt,dki->dti/dot_general | solution.py:23
  57.1 2.7 %convolution_convert_fusion.2 = bf16[64,256,128]{2,1,0:T(8,128)(2,1)S(1)} fusion(s32[64,16]{1,0:T(8,128)S(1)} %copy.28, bf16[64,16,128]{2,0,1:T(8,128)(2,1)S(1)} %get-tuple-element.42), kind=kOutput, calls=%fused_computation.10 | convolution fusion | flops 69468160 | bytes 4460544 | tf_op jit(solution)/shard_map/dkt,dki->dti/dot_general | solution.py:23
  59.9 4.7 %subtract_divide_fusion.1 = f32[64,64]{1,0:T(8,128)S(1)} fusion(bf16[64,256,128]{2,1,0:T(8,128)(2,1)S(1)} %convolution_convert_fusion.1, bf16[64,256,128]{2,1,0:T(8,128)(2,1)S(1)} %convolution_convert_fusion.2, f32[64]{0:T(128)S(1)} %get-tuple-element.45, f32[64]{0:T(128)S(1)} %get-tuple-element.41), kind=kOutput, calls=%fused_computation.40 | convolution fusion | flops 268447744 | bytes 8405504 | tf_op jit(solution)/shard_map/while/body/eval_jaxpr/dot_general | solution.py:34
  64.6 0.2 multiply_reduce_fusion
  64.7 2.9 %convolution_convert_fusion = bf16[64,256,128]{2,1,0:T(8,128)(2,1)S(1)} fusion(s32[64,16]{1,0:T(8,128)S(1)} %copy.38, bf16[64,16,128]{2,0,1:T(8,128)(2,1)S(1)} %collective-permute-done.1), kind=kOutput, calls=%fused_computation.8 | convolution fusion | flops 69468160 | bytes 4460544 | tf_op jit(solution)/shard_map/dkt,dki->dti/dot_general | solution.py:23
  67.7 4.7 %subtract_divide_fusion = f32[64,64]{1,0:T(8,128)S(1)} fusion(f32[64]{0:T(128)S(1)} %multiply_reduce_fusion, f32[64]{0:T(128)S(1)} %get-tuple-element.41, bf16[64,256,128]{2,1,0:T(8,128)(2,1)S(1)} %convolution_convert_fusion, bf16[64,256,128]{2,1,0:T(8,128)(2,1)S(1)} %convolution_convert_fusion.2), kind=kOutput, calls=%fused_computation.39 | convolution fusion | flops 268447744 | bytes 8405504 | tf_op jit(solution)/shard_map/dot_general | solution.py:34
  72.4 0.7 pad_maximum_fusion.2
  (15 shorter events, 0.5 us)
Async XLA Ops:
  7.2 13.8 %all-to-all-start = ((bf16[8,2,256]{2,1,0:T(2,128)(2,1)}), bf16[8,2,256]{2,1,0:T(2,128)(2,1)S(1)}, u32[]{:S(2)}, u32[]{:S(2)}) async-start(bf16[8,2,256]{2,1,0:T(2,128)(2,1)} %reshape.321), calls=%async_computation | async-start | bytes 16384 | tf_op jit(solution)/shard_map/all_to_all | solution.py:66
  21.0 30.8 %all-to-all-start.1 = ((bf16[8,32,16,128]{3,1,2,0:T(8,128)(2,1)}), bf16[8,32,16,128]{3,1,2,0:T(8,128)(2,1)S(1)}, u32[]{:S(2)}, u32[]{:S(2)}) async-start(bf16[8,32,16,128]{3,1,2,0:T(8,128)(2,1)} %copy.29), calls=%async_computation.1 | async-start | bytes 2097152 | tf_op jit(solution)/shard_map/all_to_all | solution.py:65
  27.4 20.6 %collective-permute-start = (bf16[64,16]{0,1:T(8,128)(2,1)S(1)}, bf16[64,16]{0,1:T(8,128)(2,1)S(1)}, u32[]{:S(2)}, u32[]{:S(2)}) collective-permute-start(bf16[64,16]{0,1:T(8,128)(2,1)S(1)} %get-tuple-element.44), channel_id=1, source_target_pairs={{28,0},{0,4},{4,8},{8,12},{12,16},{16,20},{20,24},{24,28},{29,1},{... | collective-permute-start | bytes 6152 | tf_op jit(solution)/shard_map/while/body/eval_jaxpr/ppermute | solution.py:15
  52.9 11.7 %collective-permute-start.1 = (bf16[64,16,128]{2,0,1:T(8,128)(2,1)S(1)}, bf16[64,16,128]{2,0,1:T(8,128)(2,1)S(1)}, u32[]{:S(2)}, u32[]{:S(2)}) collective-permute-start(bf16[64,16,128]{2,0,1:T(8,128)(2,1)S(1)} %get-tuple-element.46), channel_id=1, source_target_pairs={{28,0},{0,4},{4,8},{8,12},{12,16},{16,20},{20,24},{24,28},{29,1},{... | collective-permute-start | bytes 786440 | tf_op jit(solution)/shard_map/while/body/eval_jaxpr/ppermute | solution.py:15
where the time goes:
time: 73.5 us; the launch traced here: 73.1 us
  waiting for transfers between devices  22.6 us (31%)
  matrix products  18.7 us (25%)
  starting transfers between devices  16.3 us (22%)
  other arithmetic  7.92 us (11%)
  local copies, waits for them, and re-layouts  7.43 us (10%)
    ppermute x2, waiting for transfers between devices, from_behind(): return lax.ppermute(block, axis, route)  18.3 us
    dot_general x2, matrix products, similar(): lax.dot_general(own_dense, other_dense, (((1,), (1,)), ((), ())), preferr...  9.39 us
    dot_general x3, matrix products, densify(): jnp.einsum('dkt,dki->dti', selector, values, preferred_element_type=jnp.f...  8.39 us
    all_to_all x1, starting transfers between devices, deal(): lax.all_to_all(out_codes, 'rows', split_axis=0, concat_axis=0, tiled=True)  7.28 us
    all_to_all x1, starting transfers between devices, deal(): lax.all_to_all(outgoing, 'rows', split_axis=0, concat_axis=0, tiled=True)  5.42 us
    all_to_all x1, waiting for transfers between devices, deal(): lax.all_to_all(outgoing, 'rows', split_axis=0, concat_axis=0, tiled=True)  3.77 us
    ppermute x2, starting transfers between devices, from_behind(): return lax.ppermute(block, axis, route)  3.55 us
    unnamed x3, local copies, waits for them, and re-layouts  1.58 us
  transfers between devices with their start and end apart: 4, of which 3 were waited for; matrix products, arithmetic and copies ran while one was open for 24% of the time, Pallas kernels for 0%

commit v1 on v0

v1 whole, which is shorter than its diff:
```python
import functools

import jax
import jax.numpy as jnp
from jax import lax
from jax.experimental import pallas as pl
from jax.experimental.pallas import tpu as pltpu
from jax.sharding import PartitionSpec as P

MESH = pl.DeviceIdType.MESH
DOC_DEV = 64


def kernel(R, G, counts_ref, tiles_ref, vals_ref, idblk_ref, out_ref,
           staged, place, work, own, other, own_ids, other_ids,
           send_sem, recv_sem, local_sem, *inc):
    cap, K, T = vals_ref.shape
    C = staged.shape[1] - 1
    M = len(inc)
    span = M - 1
    pair = other.shape[0] // (K * DOC_DEV)
    width = pair * DOC_DEV
    me = lax.axis_index("rows")
    grp = lax.axis_index("grp")

    barrier = pltpu.get_barrier_semaphore()

    def greet(d, _):
        pl.semaphore_signal(barrier, inc=1, device_id=(lax.rem(me + d, R), grp),
                            device_id_type=MESH)
        return 0

    lax.fori_loop(1, R, greet, 0)

    def add_up(r, total):
        return total + jnp.where(r < me, counts_ref[r], 0)

    start = lax.fori_loop(0, R, add_up, jnp.int32(0), unroll=R <= 8)
    tile_line = lax.broadcasted_iota(jnp.int32, (K, T), 0)

    def stage(j, _):
        b = lax.rem(j + R - lax.rem(start, R), R)
        for a in range(C):
            s = jnp.minimum(a * R + b, cap - 1)
            block = vals_ref[s].astype(jnp.float32)
            block = jnp.where(tile_line < tiles_ref[s], block, 0.0)
            staged[j, a] = block.astype(staged.dtype)
        staged[j, C] = idblk_ref[b]
        return 0

    lax.fori_loop(0, R, stage, 0)
    pl.semaphore_wait(barrier, R - 1)

    def panel_of(row, m):
        distance = grp * span + m - 1 if m else 0
        return lax.rem(row + R - distance, R)

    def remote(m, d):
        row = lax.rem(me + d, R)
        return pltpu.make_async_remote_copy(
            src_ref=staged.at[panel_of(row, m)], dst_ref=inc[m].at[me],
            send_sem=send_sem.at[m], recv_sem=recv_sem.at[m],
            device_id=(row, grp), device_id_type=MESH)

    def send_all(m):
        def send(i, _):
            remote(m, i).start()
            return 0

        lax.fori_loop(1, R, send, 0)
        pltpu.make_async_copy(staged.at[panel_of(me, m)], inc[m].at[me],
                              local_sem.at[m]).start()

    def wait_all(m):
        pltpu.make_async_copy(staged.at[panel_of(me, m)], inc[m].at[me],
                              local_sem.at[m]).wait()
        whole = pltpu.make_async_remote_copy(
            src_ref=inc[m].at[pl.ds(0, R - 1)], dst_ref=inc[m].at[pl.ds(0, R - 1)],
            send_sem=send_sem.at[m], recv_sem=recv_sem.at[m],
            device_id=(me, grp), device_id_type=MESH)
        whole.wait_send()
        whole.wait_recv()

    for m in range(1, M):
        send_all(m)

    @pl.when(grp != 0)
    def _():
        send_all(0)

    def source_of(g):
        def look(r, carry):
            end, behind, begin = carry
            end = end + counts_ref[r]
            past = g >= end
            return (end, behind + jnp.where(past, 1, 0), jnp.where(past, end, begin))

        zero = jnp.int32(0)
        _, source, begin = lax.fori_loop(0, R, look, (zero, zero, zero), unroll=R <= 8)
        return (jnp.minimum(source, R - 1) * (C + 1)
                + jnp.minimum(lax.div(g - begin, R), C - 1))

    for m in range(M):
        anchor = panel_of(me, m)

        def note(c, _):
            place[m, c] = source_of(c * R + anchor)
            return 0

        lax.fori_loop(0, DOC_DEV, note, 0)

    lane = lax.broadcasted_iota(jnp.int32, (1, T), 1)

    def landing(anchor, shift, height):
        def fill(r, carry):
            begin, line = carry
            count = counts_ref[r]
            b = lax.rem(anchor + R - lax.rem(begin, R), R)
            slot = (lane - r * C) * R + b
            good = (lane >= r * C) & (lane < r * C + C) & (slot < count)
            return begin + count, jnp.where(good, begin + slot, line)

        _, line = lax.fori_loop(0, R, fill, (jnp.int32(0), jnp.full((1, T), -(1 << 30), jnp.int32)),
                                unroll=R <= 8)
        rows = lax.broadcasted_iota(jnp.int32, (height, T), 0) - shift
        return jnp.where(rows * R + anchor == line, 1.0, 0.0).astype(jnp.bfloat16)

    def ids_of(m):
        def add(r, total):
            return total + inc[m][r, C].astype(jnp.float32)

        return lax.fori_loop(0, R, add, jnp.zeros((K, T), jnp.float32)).astype(jnp.bfloat16)

    def compact(m, dest, shift, stride):
        flat = inc[m]

        def bring(c, _):
            at = place[m, c]
            block = flat[lax.div(at, C + 1), lax.rem(at, C + 1)]
            work[pl.ds(pl.multiple_of(c * K, K), K), :] = block.astype(jnp.float32)
            return 0

        lax.fori_loop(0, DOC_DEV, bring, 0, unroll=8)
        total = jnp.zeros((DOC_DEV, T), jnp.float32)
        for k in range(K):
            rows = work[pl.ds(k, DOC_DEV, stride=K), :]
            total = total + rows * rows
            dest[pl.ds(k * stride + shift, DOC_DEV), :] = rows.astype(dest.dtype)
        return jnp.sum(total, axis=1, keepdims=True)

    along = (((1,), (1,)), ((), ()))

    @pl.when(grp != 0)
    def _():
        wait_all(0)

    def load_own(m):
        norm = compact(m, own, 0, DOC_DEV)
        ids = lax.dot_general(landing(me, 0, DOC_DEV), ids_of(m), along,
                              preferred_element_type=jnp.float32)
        for k in range(K):
            own_ids[k] = jnp.broadcast_to(ids[:, k:k + 1], (DOC_DEV, width))
        return norm

    @pl.when(grp == 0)
    def _():
        wait_all(1)
        own_ids[K] = jnp.broadcast_to(load_own(1), (DOC_DEV, width))

    @pl.when(grp != 0)
    def _():
        own_ids[K] = jnp.broadcast_to(load_own(0), (DOC_DEV, width))
        wait_all(1)

    for m in range(2, M):
        wait_all(m)
    own_norm = own_ids[K]

    for first in range(0, span, pair):
        norms = []
        ids = jnp.zeros((K, width), jnp.float32)
        for h in range(pair):
            m = 1 + first + h
            norms.append(compact(m, other, h * DOC_DEV, width))
            ids = ids + lax.dot_general(
                ids_of(m), landing(panel_of(me, m), h * DOC_DEV, width), along,
                preferred_element_type=jnp.float32)
        other_ids[...] = ids
        norm = jnp.broadcast_to(jnp.concatenate(norms, axis=0), (width, T)).T[:DOC_DEV]

        def step(kp, acc):
            block = other[pl.ds(pl.multiple_of(kp * 2 * width, 2 * width), 2 * width), :]
            lines = [other_ids[pl.ds(2 * kp + i, 1), :] for i in range(2)]
            for quarter in range(4):
                span_k = K // 4
                rows = own[quarter * span_k * DOC_DEV:(quarter + 1) * span_k * DOC_DEV, :]
                gram = lax.dot_general(rows, block, along, preferred_element_type=jnp.float32)
                for kk in range(span_k):
                    mine = own_ids[quarter * span_k + kk]
                    for i in range(2):
                        part = gram[kk * DOC_DEV:(kk + 1) * DOC_DEV, i * width:(i + 1) * width]
                        acc = acc + jnp.where(mine == lines[i], part, 0.0)
            return acc

        product = lax.fori_loop(0, K // 2, step, jnp.zeros((DOC_DEV, width), jnp.float32))
        out_ref[:, first * DOC_DEV:first * DOC_DEV + width] = product / (
            own_norm + norm - product)


def solution(mesh):
    R, G = mesh.shape["rows"], mesh.shape["grp"]
    span = R // G
    pair = 2 if span % 2 == 0 else 1

    def on_device(tile_values, tile_ids, doc_tiles, row_counts):
        cap, K, T = tile_values.shape
        C = (cap + R - 1) // R
        me = lax.axis_index("rows")
        ids = jnp.pad(tile_ids, ((0, C * R - cap), (0, 0))).astype(jnp.bfloat16)
        ids = ids.reshape(C, R, K).transpose(1, 2, 0)
        spread = jnp.tile(ids, (1, 1, R))
        spread = jnp.where(jnp.arange(R * C) // C == me, spread, jnp.zeros((), jnp.bfloat16))
        idblk = jnp.pad(spread, ((0, 0), (0, 0), (0, T - R * C)))
        vmem = pl.BlockSpec(memory_space=pltpu.VMEM)
        smem = pl.BlockSpec(memory_space=pltpu.SMEM)
        return pl.pallas_call(
            functools.partial(kernel, R, G),
            out_shape=jax.ShapeDtypeStruct((DOC_DEV, span * DOC_DEV), jnp.float32),
            in_specs=[smem, smem, vmem, vmem],
            out_specs=vmem,
            scratch_shapes=[
                pltpu.VMEM((R, C + 1, K, T), jnp.bfloat16),
                pltpu.SMEM((span + 1, DOC_DEV), jnp.int32),
                pltpu.VMEM((DOC_DEV * K, T), jnp.float32),
                pltpu.VMEM((DOC_DEV * K, T), jnp.bfloat16),
                pltpu.VMEM((pair * DOC_DEV * K, T), jnp.bfloat16),
                pltpu.VMEM((K + 1, DOC_DEV, pair * DOC_DEV), jnp.float32),
                pltpu.VMEM((K, pair * DOC_DEV), jnp.float32),
                pltpu.SemaphoreType.DMA((span + 1,)),
                pltpu.SemaphoreType.DMA((span + 1,)),
                pltpu.SemaphoreType.DMA((span + 1,)),
            ] + [pltpu.VMEM((R, C + 1, K, T), jnp.bfloat16)] * (span + 1),
            compiler_params=pltpu.CompilerParams(collective_id=0, has_side_effects=True),
        )(row_counts, doc_tiles, tile_values, idblk)

    placed = (P("rows", None, None), P("rows", None), P("rows"), P())
    return jax.shard_map(
        on_device, mesh=mesh, in_specs=placed, out_specs=P("rows", "grp"), check_vma=False
    )
```

time: 73.5 us -> 51 us (0.69)
  the two profiles are of different devices: /device:TPU:0 before, /device:TPU:15 now
where the time goes in v1:
time: 51 us; the launch traced here: 50.8 us
  Pallas kernels  47.6 us (93%)
  local copies, waits for them, and re-layouts  2.5 us (5%)
  other arithmetic  0.64 us (1%)
    pallas_call x1, Pallas kernels, on_device(): pl.pallas_call(functools.partial(kernel, R, G), out_shape=jax.ShapeDtypeS...  47.6 us
    unnamed x2, local copies, waits for them, and re-layouts  2.17 us

profile of v1, /device:TPU:15, one launch (start us, length us, event | category | flops | bytes accessed | tf_op | source)
XLA Modules:
  0.0 50.8 jit_solution(7010699685264290233)
XLA Ops:
  0.0 0.8 %copy.6 = s32[128,16]{1,0:T(8,128)S(1)} copy(s32[128,16]{0,1:T(8,128)} %param.5) | data formatting | bytes 16384 | tf_op args[1]
  0.8 0.1 copy.7
  1.0 0.2 tile.10
  1.2 0.6 %broadcast_select_fusion.idblk_ref = bf16[8,16,128]{2,1,0:T(8,128)(2,1)} fusion(bf16[8,16,128]{2,1,0:T(8,128)(2,1)S(1)} %tile.10, pred[128]{0:T(512)(128)(4,1)S(1)} %fusion), kind=kLoop, calls=%fused_computation.1 | loop fusion | flops 16384 | bytes 65664 | tf_op jit(solution)/shard_map/jit(_where)/select_n | solution.py:222
  1.8 47.6 %shard_map.46 = f32[64,128]{1,0:T(8,128)} custom-call(s32[8]{0:T(128)} %counts_ref.1, s32[128]{0:T(128)} %tiles_ref.1, bf16[128,16,128]{2,1,0:T(8,128)(2,1)} %vals_ref.1, bf16[8,16,128]{2,1,0:T(8,128)(2,1)} %broadcast_select_fusion.idblk_ref), custom_call_target="tpu_custom_call" | custom-call | tf_op jit(solution)/shard_map/pallas_call | solution.py:226
  49.4 1.4 %copy.9 = f32[64,128]{1,0:T(8,128)} copy(f32[64,128]{1,0:T(8,128)} %shard_map.46) | data formatting | bytes 65536
  (3 shorter events, 0.1 us)

commit v2 on v1

v2 whole, which is shorter than its diff:
```python
import functools

import jax
import jax.numpy as jnp
from jax import lax
from jax.experimental import pallas as pl
from jax.experimental.pallas import tpu as pltpu
from jax.sharding import PartitionSpec as P

MESH = pl.DeviceIdType.MESH
DOC_DEV = 64
ALONG = (((1,), (1,)), ((), ()))


def kernel(R, G, counts_ref, tiles_ref, vals_ref, idblk_ref, out_ref,
           staged, inc_own, inc_peer, place, work, own, own_ids, fold,
           send_sem, recv_sem, *others):
    cap, K, T = vals_ref.shape
    H = staged.shape[1] - 1
    C = (cap + R - 1) // R
    span = len(others)
    D = DOC_DEV
    me = lax.axis_index("rows")
    grp = lax.axis_index("grp")
    core = lax.rem(grp, 2)
    peer = grp + 1 - 2 * core

    barrier = pltpu.get_barrier_semaphore()

    def greet(d, _):
        pl.semaphore_signal(barrier, inc=1, device_id=(lax.rem(me + d, R), grp),
                            device_id_type=MESH)
        return 0

    lax.fori_loop(1, R, greet, 0)
    pl.semaphore_signal(barrier, inc=1, device_id=(me, peer), device_id_type=MESH)

    def add_up(r, total):
        return total + jnp.where(r < me, counts_ref[r], 0)

    start = lax.fori_loop(0, R, add_up, jnp.int32(0), unroll=R <= 8)
    tile_line = lax.broadcasted_iota(jnp.int32, (K, T), 0)

    def stage(j, _):
        b = lax.rem(j + R - lax.rem(start, R), R)
        for h in range(H):
            s = jnp.minimum((core * H + h) * R + b, cap - 1)
            block = vals_ref[s].astype(jnp.float32)
            block = jnp.where(tile_line < tiles_ref[s], block, 0.0)
            staged[j, h] = block.astype(staged.dtype)
        staged[j, H] = idblk_ref[b]
        return 0

    lax.fori_loop(0, R, stage, 0)
    pl.semaphore_wait(barrier, R)

    def deal(d, _):
        row = lax.rem(me + d, R)
        pltpu.make_async_remote_copy(
            src_ref=staged.at[row], dst_ref=inc_own.at[me],
            send_sem=send_sem.at[0], recv_sem=recv_sem.at[0],
            device_id=(row, grp), device_id_type=MESH).start()
        return 0

    lax.fori_loop(1, R, deal, 0)
    keep = pltpu.make_async_copy(staged.at[me], inc_own.at[me], recv_sem.at[2])
    keep.start()

    def source_of(g):
        def look(r, carry):
            end, behind, begin = carry
            end = end + counts_ref[r]
            past = g >= end
            return (end, behind + jnp.where(past, 1, 0), jnp.where(past, end, begin))

        zero = jnp.int32(0)
        _, source, begin = lax.fori_loop(0, R, look, (zero, zero, zero), unroll=R <= 8)
        return jnp.minimum(source, R - 1), jnp.minimum(lax.div(g - begin, R), C - 1)

    def note(c, _):
        source, a = source_of(c * R + me)
        place[0, c] = source
        place[1, c] = a
        return 0

    lax.fori_loop(0, D, note, 0)

    lane = lax.broadcasted_iota(jnp.int32, (1, T), 1)

    def fill(r, carry):
        begin, line = carry
        count = counts_ref[r]
        b = lax.rem(me + R - lax.rem(begin, R), R)
        slot = (lane - r * C) * R + b
        good = (lane >= r * C) & (lane < r * C + C) & (slot < count)
        return begin + count, jnp.where(good, begin + slot, line)

    nowhere = jnp.full((1, T), -(1 << 30), jnp.int32)
    _, line = lax.fori_loop(0, R, fill, (jnp.int32(0), nowhere), unroll=R <= 8)

    def landing(shift):
        rows = lax.broadcasted_iota(jnp.int32, (2 * D, T), 0) - shift
        return jnp.where(rows * R + me == line, 1.0, 0.0).astype(jnp.bfloat16)

    low, high = landing(0), landing(D)

    keep.wait()
    dealt = pltpu.make_async_remote_copy(
        src_ref=staged.at[pl.ds(0, R - 1)], dst_ref=inc_own.at[pl.ds(0, R - 1)],
        send_sem=send_sem.at[0], recv_sem=recv_sem.at[0],
        device_id=(me, peer), device_id_type=MESH)
    dealt.wait_recv()
    swap = pltpu.make_async_remote_copy(
        src_ref=inc_own, dst_ref=inc_peer,
        send_sem=send_sem.at[1], recv_sem=recv_sem.at[1],
        device_id=(me, peer), device_id_type=MESH)
    swap.start()

    def add_ids(r, total):
        return total + inc_own[r, H].astype(jnp.float32)

    ids = lax.fori_loop(0, R, add_ids, jnp.zeros((K, T), jnp.float32), unroll=R <= 8)
    ids = ids.astype(jnp.bfloat16)
    mine = lax.dot_general(low, ids, ALONG, preferred_element_type=jnp.float32)
    both = [lax.dot_general(ids, hot, ALONG, preferred_element_type=jnp.float32)
            for hot in (low, high)]
    lines = both[0][:K // 2] + both[1][K // 2:]
    own[K * D:K * D + K, :] = jnp.concatenate([lines, lines], axis=0).astype(own.dtype)
    for k in range(K):
        own_ids[k] = jnp.broadcast_to(mine[:D, k:k + 1], (D, T))
    swap.wait_recv()

    def bring(c, _):
        source, a = place[0, c], place[1, c]
        ours = lax.div(a, H) == core
        h = lax.rem(a, H)
        block = jnp.where(ours, inc_own[source, h].astype(jnp.float32),
                          inc_peer[source, h].astype(jnp.float32))
        work[pl.ds(pl.multiple_of(c * K, K), K), :] = block
        return 0

    lax.fori_loop(0, D, bring, 0, unroll=8)
    total = jnp.zeros((D, T), jnp.float32)
    for k in range(K):
        rows = work[pl.ds(k, D, stride=K), :]
        total = total + rows * rows
        own[k * D:(k + 1) * D, :] = rows.astype(own.dtype)
    own_norm = jnp.broadcast_to(jnp.sum(total, axis=1, keepdims=True), (D, T))

    def outgoing(i):
        return pltpu.make_async_remote_copy(
            src_ref=own, dst_ref=others[i],
            send_sem=send_sem.at[2 + i], recv_sem=recv_sem.at[3 + i],
            device_id=(lax.rem(me + grp * span + i, R), grp), device_id_type=MESH)

    first_copy = pltpu.make_async_copy(own, others[0], recv_sem.at[3])
    for i in range(1, span):
        outgoing(i).start()

    @pl.when(grp != 0)
    def _():
        outgoing(0).start()

    @pl.when(grp == 0)
    def _():
        first_copy.start()

    def compare(i):
        other = others[i]
        fold[...] = other[K * D:K * D + K, :].astype(jnp.float32)

        def norm_part(k, total):
            rows = other[pl.ds(pl.multiple_of(k * D, D), D), :].astype(jnp.float32)
            return total + rows * rows

        total = lax.fori_loop(0, K, norm_part, jnp.zeros((D, T), jnp.float32), unroll=4)
        total = jnp.broadcast_to(jnp.sum(total, axis=1, keepdims=True), (D, T))
        norm = jnp.concatenate([total, total], axis=0).T[:D]

        def step(p, acc):
            parts = [other[pl.ds(pl.multiple_of(k * D, D), D), :]
                     for k in (2 * p, 2 * p + K // 2, 2 * p + 1, 2 * p + 1 + K // 2)]
            block = jnp.concatenate(parts, axis=0)
            marks = [fold[pl.ds(2 * p + i, 1), :] for i in range(2)]
            some = K // 4
            for quarter in range(4):
                rows = own[quarter * some * D:(quarter + 1) * some * D, :]
                gram = lax.dot_general(rows, block, ALONG, preferred_element_type=jnp.float32)
                for kk in range(some):
                    here = own_ids[quarter * some + kk]
                    for i in range(2):
                        part = gram[kk * D:(kk + 1) * D, i * T:(i + 1) * T]
                        acc = acc + jnp.where(here == marks[i], part, 0.0)
            return acc

        acc = lax.fori_loop(0, K // 4, step, jnp.zeros((D, T), jnp.float32))
        product = acc[:, :D] + acc[:, D:2 * D]
        out_ref[:, i * D:(i + 1) * D] = product / (own_norm[:, :D] + norm[:, :D] - product)

    @pl.when(grp != 0)
    def _():
        outgoing(0).wait_recv()

    @pl.when(grp == 0)
    def _():
        first_copy.wait()

    compare(0)
    for i in range(1, span):
        outgoing(i).wait_recv()
        compare(i)

    dealt.wait_send()
    swap.wait_send()
    for i in range(1, span):
        outgoing(i).wait_send()

    @pl.when(grp != 0)
    def _():
        outgoing(0).wait_send()


def solution(mesh):
    R, G = mesh.shape["rows"], mesh.shape["grp"]
    span = R // G

    def on_device(tile_values, tile_ids, doc_tiles, row_counts):
        cap, K, T = tile_values.shape
        C = (cap + R - 1) // R
        H = (C + 1) // 2
        me = lax.axis_index("rows")
        ids = jnp.pad(tile_ids, ((0, C * R - cap), (0, 0))).astype(jnp.bfloat16)
        ids = ids.reshape(C, R, K).transpose(1, 2, 0)
        spread = jnp.tile(ids, (1, 1, R))
        spread = jnp.where(jnp.arange(R * C) // C == me, spread, jnp.zeros((), jnp.bfloat16))
        idblk = jnp.pad(spread, ((0, 0), (0, 0), (0, T - R * C)))
        vmem = pl.BlockSpec(memory_space=pltpu.VMEM)
        smem = pl.BlockSpec(memory_space=pltpu.SMEM)
        panel = pltpu.VMEM((DOC_DEV * K + K, T), jnp.bfloat16)
        return pl.pallas_call(
            functools.partial(kernel, R, G),
            out_shape=jax.ShapeDtypeStruct((DOC_DEV, span * DOC_DEV), jnp.float32),
            in_specs=[smem, smem, vmem, vmem],
            out_specs=vmem,
            scratch_shapes=[
                pltpu.VMEM((R, H + 1, K, T), jnp.bfloat16),
                pltpu.VMEM((R, H + 1, K, T), jnp.bfloat16),
                pltpu.VMEM((R, H + 1, K, T), jnp.bfloat16),
                pltpu.SMEM((2, DOC_DEV), jnp.int32),
                pltpu.VMEM((DOC_DEV * K, T), jnp.float32),
                panel,
                pltpu.VMEM((K, DOC_DEV, T), jnp.float32),
                pltpu.VMEM((K, T), jnp.float32),
                pltpu.SemaphoreType.DMA((span + 2,)),
                pltpu.SemaphoreType.DMA((span + 3,)),
            ] + [panel] * span,
            compiler_params=pltpu.CompilerParams(collective_id=0, has_side_effects=True),
        )(row_counts, doc_tiles, tile_values, idblk)

    placed = (P("rows", None, None), P("rows", None), P("rows"), P())
    return jax.shard_map(
        on_device, mesh=mesh, in_specs=placed, out_specs=P("rows", "grp"), check_vma=False
    )
```

time: 51 us -> 39 us (0.76)
  the two profiles are of different devices: /device:TPU:15 before, /device:TPU:4 now
where the time goes in v2:
time: 39 us; the launch traced here: 38.8 us
  Pallas kernels  35.6 us (91%)
  local copies, waits for them, and re-layouts  2.5 us (6%)
  other arithmetic  0.64 us (2%)
    pallas_call x1, Pallas kernels, on_device(): pl.pallas_call(functools.partial(kernel, R, G), out_shape=jax.ShapeDtypeS...  35.6 us
    unnamed x2, local copies, waits for them, and re-layouts  2.17 us

profile of v2, /device:TPU:4, one launch (start us, length us, event | category | flops | bytes accessed | tf_op | source)
XLA Modules:
  0.0 38.8 jit_solution(7935948527603528387)
XLA Ops:
  0.0 0.8 %copy.6 = s32[128,16]{1,0:T(8,128)S(1)} copy(s32[128,16]{0,1:T(8,128)} %param.5) | data formatting | bytes 16384 | tf_op args[1]
  0.8 0.1 copy.7
  1.0 0.2 tile.10
  1.2 0.6 %broadcast_select_fusion.idblk_ref = bf16[8,16,128]{2,1,0:T(8,128)(2,1)} fusion(bf16[8,16,128]{2,1,0:T(8,128)(2,1)S(1)} %tile.10, pred[128]{0:T(512)(128)(4,1)S(1)} %fusion), kind=kLoop, calls=%fused_computation.1 | loop fusion | flops 16384 | bytes 65664 | tf_op jit(solution)/shard_map/jit(_where)/select_n | solution.py:235
  1.8 35.6 %shard_map.46 = f32[64,128]{1,0:T(8,128)} custom-call(s32[8]{0:T(128)} %counts_ref.1, s32[128]{0:T(128)} %tiles_ref.1, bf16[128,16,128]{2,1,0:T(8,128)(2,1)} %vals_ref.1, bf16[8,16,128]{2,1,0:T(8,128)(2,1)} %broadcast_select_fusion.idblk_ref), custom_call_target="tpu_custom_call" | custom-call | tf_op jit(solution)/shard_map/pallas_call | solution.py:240
  37.4 1.4 %copy.9 = f32[64,128]{1,0:T(8,128)} copy(f32[64,128]{1,0:T(8,128)} %shard_map.46) | data formatting | bytes 65536
  (3 shorter events, 0.1 us)

commit v3 on v2

--- a/solution.py
+++ b/solution.py
@@ -14,7 +14,7 @@
 
 def kernel(R, G, counts_ref, tiles_ref, vals_ref, idblk_ref, out_ref,
            staged, inc_own, inc_peer, place, work, own, own_ids, fold,
-           send_sem, recv_sem, *others):
+           vals, vals_sem, ahead, back, send_sem, recv_sem, give_sem, take_sem, *others):
     cap, K, T = vals_ref.shape
     H = staged.shape[1] - 1
     C = (cap + R - 1) // R
@@ -25,6 +25,10 @@
     core = lax.rem(grp, 2)
     peer = grp + 1 - 2 * core
 
+    window = vals.shape[0]
+    base = jnp.minimum(core * window, cap - window)
+    fetch = pltpu.make_async_copy(vals_ref.at[pl.ds(base, window)], vals, vals_sem)
+    fetch.start()
     barrier = pltpu.get_barrier_semaphore()
 
     def greet(d, _):
@@ -34,6 +38,26 @@
 
     lax.fori_loop(1, R, greet, 0)
     pl.semaphore_signal(barrier, inc=1, device_id=(me, peer), device_id_type=MESH)
+    order = range(span - 1, -1, -1)
+
+    def distance(i):
+        return grp * span + i
+
+    def formed(i):
+        k = distance(i)
+        return (k == 0) | ((k >= span) & (2 * k <= R)) | (k > R - span)
+
+    def given(i):
+        k = distance(i)
+        return formed(i) & (k != 0) & (2 * k != R)
+
+    for i in range(span):
+        k = R - distance(i)
+
+        @pl.when(jnp.logical_not(formed(i)))
+        def _():
+            pl.semaphore_signal(barrier, inc=1, device_id=(lax.rem(me + k, R), lax.div(k, span)),
+                                device_id_type=MESH)
 
     def add_up(r, total):
         return total + jnp.where(r < me, counts_ref[r], 0)
@@ -45,14 +69,16 @@
         b = lax.rem(j + R - lax.rem(start, R), R)
         for h in range(H):
             s = jnp.minimum((core * H + h) * R + b, cap - 1)
-            block = vals_ref[s].astype(jnp.float32)
+            block = vals[s - base].astype(jnp.float32)
             block = jnp.where(tile_line < tiles_ref[s], block, 0.0)
             staged[j, h] = block.astype(staged.dtype)
         staged[j, H] = idblk_ref[b]
         return 0
 
+    fetch.wait()
     lax.fori_loop(0, R, stage, 0)
-    pl.semaphore_wait(barrier, R)
+    givers = sum(jnp.where(given(i), 1, 0) for i in range(span))
+    pl.semaphore_wait(barrier, R + givers)
 
     def deal(d, _):
         row = lax.rem(me + d, R)
@@ -154,16 +180,29 @@
             device_id=(lax.rem(me + grp * span + i, R), grp), device_id_type=MESH)
 
     first_copy = pltpu.make_async_copy(own, others[0], recv_sem.at[3])
-    for i in range(1, span):
-        outgoing(i).start()
-
-    @pl.when(grp != 0)
-    def _():
-        outgoing(0).start()
+
+    def when_travels(i, act):
+        k = distance(i)
+
+        @pl.when((k != 0) & formed(i))
+        def _():
+            act(outgoing(i))
+
+    for i in order:
+        when_travels(i, lambda copy: copy.start())
 
     @pl.when(grp == 0)
     def _():
         first_copy.start()
+
+    def giving(i):
+        k = distance(i)
+        twin = R - k
+        j = (span - i) % span
+        return pltpu.make_async_remote_copy(
+            src_ref=ahead.at[i], dst_ref=back.at[j],
+            send_sem=give_sem.at[i], recv_sem=take_sem.at[j],
+            device_id=(lax.rem(me + twin, R), lax.div(twin, span)), device_id_type=MESH)
 
     def compare(i):
         other = others[i]
@@ -195,29 +234,47 @@
 
         acc = lax.fori_loop(0, K // 4, step, jnp.zeros((D, T), jnp.float32))
         product = acc[:, :D] + acc[:, D:2 * D]
-        out_ref[:, i * D:(i + 1) * D] = product / (own_norm[:, :D] + norm[:, :D] - product)
-
-    @pl.when(grp != 0)
-    def _():
-        outgoing(0).wait_recv()
-
-    @pl.when(grp == 0)
-    def _():
-        first_copy.wait()
-
-    compare(0)
-    for i in range(1, span):
-        outgoing(i).wait_recv()
-        compare(i)
+        block = product / (own_norm[:, :D] + norm[:, :D] - product)
+        wide = jnp.concatenate([block, block], axis=1)
+        ahead[i] = jnp.concatenate([wide, wide], axis=0).T[:D]
+        out_ref[:, i * D:(i + 1) * D] = block
+
+    for i in order:
+        k = distance(i)
+        if i == 0:
+            @pl.when(grp == 0)
+            def _():
+                first_copy.wait()
+
+        when_travels(i, lambda copy: copy.wait_recv())
+
+        @pl.when(formed(i))
+        def _():
+            compare(i)
+
+        @pl.when(given(i))
+        def _():
+            giving(i).start()
+
+    for i in order:
+        k = distance(i)
+
+        @pl.when(jnp.logical_not(formed(i)))
+        def _():
+            pltpu.make_async_remote_copy(
+                src_ref=ahead.at[i], dst_ref=back.at[i],
+                send_sem=give_sem.at[i], recv_sem=take_sem.at[i],
+                device_id=(me, peer), device_id_type=MESH).wait_recv()
+            out_ref[:, i * D:(i + 1) * D] = back[i][:, :D]
+
+        @pl.when(given(i))
+        def _():
+            giving(i).wait_send()
+
+        when_travels(i, lambda copy: copy.wait_send())
 
     dealt.wait_send()
     swap.wait_send()
-    for i in range(1, span):
-        outgoing(i).wait_send()
-
-    @pl.when(grp != 0)
-    def _():
-        outgoing(0).wait_send()
 
 
 def solution(mesh):
@@ -240,7 +297,7 @@
         return pl.pallas_call(
             functools.partial(kernel, R, G),
             out_shape=jax.ShapeDtypeStruct((DOC_DEV, span * DOC_DEV), jnp.float32),
-            in_specs=[smem, smem, vmem, vmem],
+            in_specs=[smem, smem, pl.BlockSpec(memory_space=pl.ANY), vmem],
             out_specs=vmem,
             scratch_shapes=[
                 pltpu.VMEM((R, H + 1, K, T), jnp.bfloat16),
@@ -251,8 +308,14 @@
                 panel,
                 pltpu.VMEM((K, DOC_DEV, T), jnp.float32),
                 pltpu.VMEM((K, T), jnp.float32),
+                pltpu.VMEM((min(H * R, cap), K, T), jnp.bfloat16),
+                pltpu.SemaphoreType.DMA,
+                pltpu.VMEM((span, DOC_DEV, T), jnp.float32),
+                pltpu.VMEM((span, DOC_DEV, T), jnp.float32),
                 pltpu.SemaphoreType.DMA((span + 2,)),
                 pltpu.SemaphoreType.DMA((span + 3,)),
+                pltpu.SemaphoreType.DMA((span,)),
+                pltpu.SemaphoreType.DMA((span,)),
             ] + [panel] * span,
             compiler_params=pltpu.CompilerParams(collective_id=0, has_side_effects=True),
         )(row_counts, doc_tiles, tile_values, idblk)

time: 39 us -> 35.5 us (0.910)
  the two profiles are of different devices: /device:TPU:4 before, /device:TPU:1 now
where the time goes in v3:
time: 35.5 us; the launch traced here: 35.2 us
  Pallas kernels  32 us (90%)
  local copies, waits for them, and re-layouts  2.5 us (7%)
  other arithmetic  0.64 us (2%)
    pallas_call x1, Pallas kernels, on_device(): pl.pallas_call(functools.partial(kernel, R, G), out_shape=jax.ShapeDtypeS...  32 us
    unnamed x2, local copies, waits for them, and re-layouts  2.17 us

profile of v3, /device:TPU:1, one launch (start us, length us, event | category | flops | bytes accessed | tf_op | source)
XLA Modules:
  0.0 35.2 jit_solution(15694640826770456741)
XLA Ops:
  0.0 0.8 %copy.6 = s32[128,16]{1,0:T(8,128)S(1)} copy(s32[128,16]{0,1:T(8,128)} %param.5) | data formatting | bytes 16384 | tf_op args[1]
  0.8 0.1 copy.7
  1.0 0.2 tile.10
  1.2 0.6 %broadcast_select_fusion.idblk_ref = bf16[8,16,128]{2,1,0:T(8,128)(2,1)} fusion(bf16[8,16,128]{2,1,0:T(8,128)(2,1)S(1)} %tile.10, pred[128]{0:T(512)(128)(4,1)S(1)} %fusion), kind=kLoop, calls=%fused_computation.1 | loop fusion | flops 16384 | bytes 65664 | tf_op jit(solution)/shard_map/jit(_where)/select_n | solution.py:292
  1.8 32.0 %shard_map.46 = f32[64,128]{1,0:T(8,128)} custom-call(s32[8]{0:T(128)} %counts_ref.1, s32[128]{0:T(128)} %tiles_ref.1, bf16[128,16,128]{2,1,0:T(8,128)(2,1)} %vals_ref.1, bf16[8,16,128]{2,1,0:T(8,128)(2,1)} %broadcast_select_fusion.idblk_ref), custom_call_target="tpu_custom_call" | custom-call | tf_op jit(solution)/shard_map/pallas_call | solution.py:297
  33.8 1.4 %copy.9 = f32[64,128]{1,0:T(8,128)} copy(f32[64,128]{1,0:T(8,128)} %shard_map.46) | data formatting | bytes 65536
  (3 shorter events, 0.1 us)
